TPU v7x, 32 devices: a whole 2x2x4 slice. The times are simulated.
32 devices in a mesh: seq: 16 (over z, y, core), head: 2 (over x).
Axes of the slice: x: 2, y: 2, z: 4, core: 2. Of those that a mesh axis runs over, the one named last changes fastest.
Arguments:
- query: bfloat16 [4096, 2048], P('seq', 'head'), may hold values from -4.5 to 4.5
- key_value: bfloat16 [4096, 512], P('seq'), may hold values from -4.5 to 4.5
- out_grad: bfloat16 [4096, 2048], P('seq', 'head'), may hold values from -48 to 48
- inputs_normed: bfloat16 [4096, 4096], P('seq'), may hold values from -8 to 8
- kv_weight: bfloat16 [2, 4096, 256], P(None, 'head'), may hold values from -0.09375 to 0.09375
- segment_ids: int32 [4096], replicated, may hold values from 0 to 2, never falling along the last dimension, each value on 1 to 2048 neighbouring positions
Outputs:
- query_grad: bfloat16 [4096, 2048], P('seq', 'head')
- input_grad: bfloat16 [4096, 4096], P('seq', 'head')
- weight_grad: float32 [2, 4096, 256], P('head', 'seq')
All inputs are finite; a program needn't handle non-finite values.
Results may differ from a plain program's by a relative error of at most 0.015.
Values may be sent and summed in bfloat16 or wider, within the bound.
A program may use at most 64 MiB of HBM per device.

v0:
```python
import math

import jax
import jax.numpy as jnp
from jax import lax
from jax.sharding import PartitionSpec as P

WIN = 2048


def passed_along(value, axis, steps):
    count = lax.axis_size(axis)
    leading, last = (max(0, -steps), min(count, count - steps))
    return lax.ppermute(value, axis, [(source, source + steps) for source in range(leading, last)])


def attention_block(query_rows, out_rows, window, allowed, head_count):
    head_dim = window.shape[1] // 2
    tok_rows = query_rows.shape[0]
    inv_root = 1.0 / math.sqrt(head_dim)
    key_rows = window[:, :head_dim]
    value_rows = window[:, head_dim:]
    flat_q = query_rows.reshape(tok_rows * head_count, head_dim)
    flat_do = out_rows.reshape(tok_rows * head_count, head_dim)
    scores = jnp.dot(flat_q, key_rows.T, preferred_element_type=jnp.float32) * inv_root
    scores = scores.reshape(tok_rows, head_count, -1)
    masked = jnp.where(allowed[:, None, :], scores, -jnp.inf)
    row_max = jnp.max(masked, axis=-1, keepdims=True)
    shifted = jnp.exp(masked - row_max)
    probabilities = (shifted / jnp.sum(shifted, axis=-1, keepdims=True)).reshape(
        tok_rows * head_count, -1
    )
    prob_bf16 = probabilities.astype(jnp.bfloat16)
    attended = jnp.dot(prob_bf16, value_rows, preferred_element_type=jnp.float32)
    row_delta = jnp.sum(flat_do.astype(jnp.float32) * attended, axis=-1, keepdims=True)
    prob_grad = jnp.dot(flat_do, value_rows.T, preferred_element_type=jnp.float32)
    dscore_b = (probabilities * (prob_grad - row_delta)).astype(jnp.bfloat16)
    query_grad = (
        jnp.dot(dscore_b, key_rows, preferred_element_type=jnp.float32) * inv_root
    ).astype(jnp.bfloat16)
    query_grad = query_grad.reshape(tok_rows, head_count * head_dim)
    key_grad = jnp.dot(dscore_b.T, flat_q, preferred_element_type=jnp.float32) * inv_root
    value_grad = jnp.dot(prob_bf16.T, flat_do, preferred_element_type=jnp.float32)
    return (query_grad, jnp.concatenate([key_grad, value_grad], axis=1))


def gather_window(local_kv, reach_blocks):
    received = []
    for hop_count in range(reach_blocks, 0, -1):
        received.append(passed_along(local_kv, "seq", hop_count))
    return jnp.concatenate(received + [local_kv], axis=0)


def return_grads(grad_parts, reach_blocks):
    summed = grad_parts[0]
    for distance in range(1, reach_blocks + 1):
        summed = summed + passed_along(
            grad_parts[distance].astype(jnp.bfloat16), "seq", -distance
        ).astype(jnp.float32)
    return summed


def local(query, key_value, out_grad, inputs_normed, kv_weight, segment_ids):
    tok_rows = query.shape[0]
    head_dim = key_value.shape[1] // 2
    local_heads = query.shape[1] // head_dim
    reach_blocks = WIN // tok_rows
    span = WIN + tok_rows
    seq_index = lax.axis_index("seq")
    window = gather_window(key_value, reach_blocks)
    padded_seg = jnp.concatenate([jnp.full((WIN,), -1, jnp.int32), segment_ids], axis=0)
    begin_row = seq_index * tok_rows
    key_seg = lax.dynamic_slice_in_dim(padded_seg, begin_row, span, 0)
    query_seg = lax.dynamic_slice_in_dim(segment_ids, begin_row, tok_rows, 0)
    query_pos = begin_row + jnp.arange(tok_rows, dtype=jnp.int32)
    key_pos = begin_row - WIN + jnp.arange(span, dtype=jnp.int32)
    distance = query_pos[:, None] - key_pos[None, :]
    allowed = (distance >= 0) & (distance < WIN) & (query_seg[:, None] == key_seg[None, :])
    query_grad, window_grad = attention_block(query, out_grad, window, allowed, local_heads)
    blocks = window_grad.reshape(reach_blocks + 1, tok_rows, 2 * head_dim)
    halves = lax.psum_scatter(
        blocks.astype(jnp.bfloat16), "head", scatter_dimension=2, tiled=True
    ).astype(jnp.float32)
    own_grad = return_grads(
        [halves[reach_blocks - gap_blocks] for gap_blocks in range(reach_blocks + 1)], reach_blocks
    )
    my_half = own_grad.astype(jnp.bfloat16)
    both_halves = lax.all_gather(my_half, "head", axis=1, tiled=True)
    stacked_weight = jnp.concatenate([kv_weight[0], kv_weight[1]], axis=1)
    input_grad = jnp.einsum(
        "tc,dc->td", both_halves, stacked_weight, preferred_element_type=jnp.float32
    ).astype(jnp.bfloat16)
    norm_factor = 1.0 / math.sqrt(tok_rows * lax.axis_size("seq"))
    weight_part = lax.psum_scatter(
        jnp.einsum("tr,tc->rc", inputs_normed, my_half, preferred_element_type=jnp.float32)
        * norm_factor,
        "seq",
        scatter_dimension=0,
        tiled=True,
    )
    return (query_grad, input_grad, weight_part[None])


def solution(mesh):
    return jax.shard_map(
        local,
        mesh=mesh,
        in_specs=(
            P("seq", "head"),
            P("seq", None),
            P("seq", "head"),
            P("seq", None),
            P(None, "head", None),
            P(),
        ),
        out_specs=(P("seq", "head"), P("seq", "head"), P("head", "seq", None)),
        check_vma=False,
    )
```

profile of v0, /device:TPU:13, one launch (start us, length us, event | category | flops | bytes accessed | tf_op | source)
XLA Modules:
  0.0 247.2 jit_solution(9114608913827746097)
XLA Ops:
  7.2 5.1 %collective-permute-start = (bf16[256,512]{1,0:T(8,128)(2,1)}, bf16[256,512]{1,0:T(8,128)(2,1)}, u32[]{:S(2)}, u32[]{:S(2)}) collective-permute-start(bf16[256,512]{1,0:T(8,128)(2,1)} %param.7), channel_id=1, source_target_pairs={{0,16},{2,18},{4,20},{6,22},{8,24},{10,26},{12,28},{14,30},{1,17},... | collective-permute-start | bytes 786440 | tf_op jit(solution)/shard_map/ppermute | solution.py:14
  12.3 1.9 collective-permute-start.1
  14.2 1.9 collective-permute-start.2
  16.1 1.9 collective-permute-start.3
  18.1 1.9 collective-permute-start.4
  20.0 0.8 dynamic_slice.6
  20.8 0.8 pad_dynamic-slice_fusion
  21.6 0.9 fusion.7
  22.5 3.5 %broadcast_in_dim.16 = pred[256,4,2304]{2,1,0:T(4,128)(4,1)} broadcast(pred[256,2304]{1,0:T(8,128)(4,1)S(1)} %fusion.7), dimensions={0,2} | broadcast | bytes 2949120 | tf_op jit(solution)/shard_map/jit(_where)/broadcast_in_dim | solution.py:27
  26.0 6.8 %broadcast_in_dim.17 = pred[1024,2304]{1,0:T(32,128)(4,1)} reshape(pred[256,4,2304]{2,1,0:T(4,128)(4,1)} %broadcast_in_dim.16) | data formatting | bytes 4718592 | tf_op jit(solution)/shard_map/jit(_where)/broadcast_in_dim | solution.py:27
  32.8 5.5 %copy.18 = pred[1024,2304]{0,1:T(32,128)(4,1)} copy(pred[1024,2304]{1,0:T(32,128)(4,1)} %broadcast_in_dim.17) | data formatting | bytes 4718592 | tf_op jit(solution)/shard_map/jit(_where)/broadcast_in_dim | solution.py:27
  38.4 1.1 reshape.101
  39.5 0.3 reshape.102
  39.8 0.2 copy.19
  40.1 2.2 collective-permute-start.5
  42.3 1.0 constant_dynamic-update-slice_fusion.8
  43.3 1.9 collective-permute-start.6
  45.2 1.0 constant_dynamic-update-slice_fusion.7
  46.2 2.6 %collective-permute-done.2 = bf16[256,512]{1,0:T(8,128)(2,1)} collective-permute-done((bf16[256,512]{1,0:T(8,128)(2,1)}, bf16[256,512]{1,0:T(8,128)(2,1)}, u32[]{:S(2)}, u32[]{:S(2)}) %collective-permute-start.2) | collective-permute-done | bytes 262176 | tf_op jit(solution)/shard_map/ppermute | solution.py:14
  48.7 2.1 collective-permute-start.7
  50.8 1.0 constant_dynamic-update-slice_fusion.6
  51.8 2.5 %collective-permute-done.3 = bf16[256,512]{1,0:T(8,128)(2,1)} collective-permute-done((bf16[256,512]{1,0:T(8,128)(2,1)}, bf16[256,512]{1,0:T(8,128)(2,1)}, u32[]{:S(2)}, u32[]{:S(2)}) %collective-permute-start.3) | collective-permute-done | bytes 262176 | tf_op jit(solution)/shard_map/ppermute | solution.py:14
  54.4 1.0 constant_dynamic-update-slice_fusion.5
  55.3 4.6 %collective-permute-done.4 = bf16[256,512]{1,0:T(8,128)(2,1)} collective-permute-done((bf16[256,512]{1,0:T(8,128)(2,1)}, bf16[256,512]{1,0:T(8,128)(2,1)}, u32[]{:S(2)}, u32[]{:S(2)}) %collective-permute-start.4) | collective-permute-done | bytes 262176 | tf_op jit(solution)/shard_map/ppermute | solution.py:14
  60.0 1.0 constant_dynamic-update-slice_fusion.4
  60.9 4.5 %collective-permute-done.5 = bf16[256,512]{1,0:T(8,128)(2,1)S(1)} collective-permute-done((bf16[256,512]{1,0:T(8,128)(2,1)S(1)}, bf16[256,512]{1,0:T(8,128)(2,1)S(1)}, u32[]{:S(2)}, u32[]{:S(2)}) %collective-permute-start.5) | collective-permute-done | bytes 262176 | tf_op jit(solution)/shard_map/ppermute | solution.py:14
  65.5 5.6 %collective-permute-done.6 = bf16[256,512]{1,0:T(8,128)(2,1)S(1)} collective-permute-done((bf16[256,512]{1,0:T(8,128)(2,1)S(1)}, bf16[256,512]{1,0:T(8,128)(2,1)S(1)}, u32[]{:S(2)}, u32[]{:S(2)}) %collective-permute-start.6) | collective-permute-done | bytes 262176 | tf_op jit(solution)/shard_map/ppermute | solution.py:14
  71.1 2.9 %collective-permute-done.7 = bf16[256,512]{1,0:T(8,128)(2,1)S(1)} collective-permute-done((bf16[256,512]{1,0:T(8,128)(2,1)S(1)}, bf16[256,512]{1,0:T(8,128)(2,1)S(1)}, u32[]{:S(2)}, u32[]{:S(2)}) %collective-permute-start.7) | collective-permute-done | bytes 262176 | tf_op jit(solution)/shard_map/ppermute | solution.py:14
  74.1 1.8 fusion.26
  75.9 1.3 fusion.2
  77.2 1.7 fusion.5
  78.9 1.5 convolution_convert_fusion
  80.4 0.1 copy-done.7
  80.5 1.5 fusion.12
  82.0 2.5 fusion
  84.5 1.5 fusion.4
  86.0 0.6 copy-done.9
  86.6 1.6 pad_maximum_fusion
  88.1 4.3 %copy.20 = bf16[2304,512]{1,0:T(8,128)(2,1)} copy(bf16[2304,512]{0,1:T(8,128)(2,1)} %pad_maximum_fusion) | data formatting | bytes 4718592 | tf_op jit(solution)/shard_map/concatenate | solution.py:44
  92.5 35.5 %reduce-scatter.3.cloned.1.call-done = bf16[9,256,256]{2,1,0:T(8,128)(2,1)} async-done(((bf16[9,256,512]{2,1,0:T(8,128)(2,1)}), bf16[9,256,256]{2,1,0:T(8,128)(2,1)}) %reduce-scatter.3.cloned.1.call-update) | async-done | bytes 1179664 | tf_op jit(solution)/shard_map/reduce_scatter | solution.py:81
  128.0 1.4 slice_bitcast_fusion.9
  129.4 2.9 %collective-permute-start.10 = (bf16[256,256]{1,0:T(8,128)(2,1)S(1)}, bf16[256,256]{1,0:T(8,128)(2,1)S(1)}, u32[]{:S(2)}, u32[]{:S(2)}) collective-permute-start(bf16[256,256]{1,0:T(8,128)(2,1)S(1)} %get-tuple-element.17), channel_id=1, source_target_pairs={{6,0},{8,2},{10,4},{12,6},{14,8},{16,10},{18,12},{20,14},{22,16},{... | collective-permute-start | bytes 393224 | tf_op jit(solution)/shard_map/ppermute | solution.py:14
  132.3 2.2 collective-permute-start.11
  134.5 1.9 collective-permute-start.12
  136.4 1.9 collective-permute-start.13
  138.3 1.9 collective-permute-start.14
  140.3 1.3 collective-permute-start.15
  141.6 1.9 collective-permute-start.8
  143.5 0.6 collective-permute-done.12
  144.0 2.1 collective-permute-start.9
  146.2 0.6 collective-permute-done.13
  146.7 2.8 %collective-permute-done.14 = bf16[256,256]{1,0:T(8,128)(2,1)S(1)} collective-permute-done((bf16[256,256]{1,0:T(8,128)(2,1)S(1)}, bf16[256,256]{1,0:T(8,128)(2,1)S(1)}, u32[]{:S(2)}, u32[]{:S(2)}) %collective-permute-start.14) | collective-permute-done | bytes 131104 | tf_op jit(solution)/shard_map/ppermute | solution.py:14
  149.5 1.7 collective-permute-done.15
  151.3 12.3 %collective-permute-done.8 = bf16[256,256]{1,0:T(8,128)(2,1)S(1)} collective-permute-done((bf16[256,256]{1,0:T(8,128)(2,1)S(1)}, bf16[256,256]{1,0:T(8,128)(2,1)S(1)}, u32[]{:S(2)}, u32[]{:S(2)}) %collective-permute-start.8) | collective-permute-done | bytes 131104 | tf_op jit(solution)/shard_map/ppermute | solution.py:14
  163.6 1.0 collective-permute-done.9
  164.6 1.1 fusion.24
  165.7 2.8 %fusion.3 = f32[4096,256]{0,1:T(8,128)} fusion(bf16[256,256]{1,0:T(8,128)(2,1)S(1)} %fusion.24, bf16[256,4096]{1,0:T(8,128)(2,1)S(1)} %copy-done), kind=kOutput, calls=%fused_computation.7 | convolution fusion | flops 537919488 | bytes 6422528 | tf_op jit(solution)/shard_map/tr,tc->rc/dot_general | solution.py:95
  168.5 2.8 %slice_bitcast_fusion.1 = (bf16[2048,256]{1,0:T(8,128)(2,1)S(1)}, bf16[2048,256]{1,0:T(8,128)(2,1)}) fusion(bf16[2,2048,256]{2,1,0:T(8,128)(2,1)} %param.10), kind=kLoop, calls=%fused_computation.26 | loop fusion | bytes 4194304 | tf_op jit(solution)/shard_map/squeeze | solution.py:89
  171.4 4.6 %fusion.11 = bf16[1024,256]{1,0:T(8,128)(2,1)} fusion(bf16[1024,2304]{0,1:T(8,128)(2,1)} %copy-done.9, bf16[2304,512]{1,0:T(8,128)(2,1)S(1)} %copy-done.8), kind=kOutput, calls=%fused_computation.23 | convolution fusion | flops 1208483840 | bytes 6422528 | tf_op jit(solution)/shard_map/dot_general | solution.py:39
  175.9 2.2 reshape.103
  178.1 4.5 %all_gather.3 = bf16[256,512]{1,0:T(8,128)(2,1)S(1)} all-gather(bf16[256,256]{1,0:T(8,128)(2,1)S(1)} %fusion.24), channel_id=1, replica_groups=mesh['seq'=16,'head'=2] {'head'}, dimensions={1}, use_global_device_ids=true | all-gather | bytes 393216 | tf_op jit(solution)/shard_map/all_gather | solution.py:88
  182.6 3.0 %convolution_convert_fusion.1 = bf16[256,2048]{1,0:T(8,128)(2,1)} fusion(bf16[256,512]{1,0:T(8,128)(2,1)S(1)} %all_gather.3, bf16[2048,256]{1,0:T(8,128)(2,1)} %get-tuple-element.10, bf16[2048,256]{1,0:T(8,128)(2,1)S(1)} %get-tuple-element.9), kind=kOutput, calls=%fused_computation.14 | convolution fusion | flops 541589504 | bytes 3407872 | tf_op jit(solution)/shard_map/tc,dc->td/dot_general | solution.py:90
  185.6 53.0 %reduce-scatter.5.cloned.1.call-done = f32[256,256]{0,1:T(8,128)} async-done(((f32[4096,256]{0,1:T(8,128)}), f32[256,256]{0,1:T(8,128)}) %reduce-scatter.5.cloned.1.call-update) | async-done | bytes 262160 | tf_op jit(solution)/shard_map/reduce_scatter | solution.py:94
  238.5 1.8 copy.21
  (31 shorter events, 0.2 us)
Async XLA Ops:
  7.2 158.5 %copy-start = (bf16[256,4096]{1,0:T(8,128)(2,1)S(1)}, bf16[256,4096]{1,0:T(8,128)(2,1)}, u32[]{:S(2)}) copy-start(bf16[256,4096]{1,0:T(8,128)(2,1)} %param.9) | copy-start | bytes 6291460
  7.2 120.8 %reduce-scatter.3.cloned.1.call-start = ((), (), s32[]{:S(2)}) async-start(), calls=%async_computation.2 | async-start | bytes 3538944 | tf_op jit(solution)/shard_map/reduce_scatter | solution.py:81
  7.2 32.8 %collective-permute-start = (bf16[256,512]{1,0:T(8,128)(2,1)}, bf16[256,512]{1,0:T(8,128)(2,1)}, u32[]{:S(2)}, u32[]{:S(2)}) collective-permute-start(bf16[256,512]{1,0:T(8,128)(2,1)} %param.7), channel_id=1, source_target_pairs={{0,16},{2,18},{4,20},{6,22},{8,24},{10,26},{12,28},{14,30},{1,17},... | collective-permute-start | bytes 786440 | tf_op jit(solution)/shard_map/ppermute | solution.py:14
  12.3 31.0 %collective-permute-start.1 = (bf16[256,512]{1,0:T(8,128)(2,1)}, bf16[256,512]{1,0:T(8,128)(2,1)}, u32[]{:S(2)}, u32[]{:S(2)}) collective-permute-start(bf16[256,512]{1,0:T(8,128)(2,1)} %param.7), channel_id=1, source_target_pairs={{0,14},{2,16},{4,18},{6,20},{8,22},{10,24},{12,26},{14,28},{16,30}... | collective-permute-start | bytes 786440 | tf_op jit(solution)/shard_map/ppermute | solution.py:14
  14.2 34.5 %collective-permute-start.2 = (bf16[256,512]{1,0:T(8,128)(2,1)}, bf16[256,512]{1,0:T(8,128)(2,1)}, u32[]{:S(2)}, u32[]{:S(2)}) collective-permute-start(bf16[256,512]{1,0:T(8,128)(2,1)} %param.7), channel_id=1, source_target_pairs={{0,12},{2,14},{4,16},{6,18},{8,20},{10,22},{12,24},{14,26},{16,28}... | collective-permute-start | bytes 786440 | tf_op jit(solution)/shard_map/ppermute | solution.py:14
  16.1 38.2 %collective-permute-start.3 = (bf16[256,512]{1,0:T(8,128)(2,1)}, bf16[256,512]{1,0:T(8,128)(2,1)}, u32[]{:S(2)}, u32[]{:S(2)}) collective-permute-start(bf16[256,512]{1,0:T(8,128)(2,1)} %param.7), channel_id=1, source_target_pairs={{0,10},{2,12},{4,14},{6,16},{8,18},{10,20},{12,22},{14,24},{16,26}... | collective-permute-start | bytes 786440 | tf_op jit(solution)/shard_map/ppermute | solution.py:14
  18.1 41.9 %collective-permute-start.4 = (bf16[256,512]{1,0:T(8,128)(2,1)}, bf16[256,512]{1,0:T(8,128)(2,1)}, u32[]{:S(2)}, u32[]{:S(2)}) collective-permute-start(bf16[256,512]{1,0:T(8,128)(2,1)} %param.7), channel_id=1, source_target_pairs={{0,8},{2,10},{4,12},{6,14},{8,16},{10,18},{12,20},{14,22},{16,24},... | collective-permute-start | bytes 786440 | tf_op jit(solution)/shard_map/ppermute | solution.py:14
  32.8 5.6 %copy-start.2 = (bf16[256,1024]{1,0:T(8,128)(2,1)S(1)}, bf16[256,1024]{1,0:T(8,128)(2,1)}, u32[]{:S(2)}) copy-start(bf16[256,1024]{1,0:T(8,128)(2,1)} %param.6) | copy-start | bytes 1572868
  32.8 6.7 %copy-start.3 = (bf16[256,1024]{1,0:T(8,128)(2,1)S(1)}, bf16[256,1024]{1,0:T(8,128)(2,1)}, u32[]{:S(2)}) copy-start(bf16[256,1024]{1,0:T(8,128)(2,1)} %param.8) | copy-start | bytes 1572868
  38.4 1.7 copy-start.5
  40.0 34.0 %copy-start.1 = (pred[1024,2304]{0,1:T(32,128)(4,1)S(1)}, pred[1024,2304]{0,1:T(32,128)(4,1)}, u32[]{:S(2)}) copy-start(pred[1024,2304]{0,1:T(32,128)(4,1)} %copy.18) | copy-start | bytes 7077892
  40.0 34.0 %copy-start.4 = (bf16[1024,256]{1,0:T(8,128)(2,1)S(1)}, bf16[1024,256]{1,0:T(8,128)(2,1)}, u32[]{:S(2)}) copy-start(bf16[1024,256]{1,0:T(8,128)(2,1)} %reshape.101) | copy-start | bytes 1572868
  40.1 25.4 %collective-permute-start.5 = (bf16[256,512]{1,0:T(8,128)(2,1)S(1)}, bf16[256,512]{1,0:T(8,128)(2,1)S(1)}, u32[]{:S(2)}, u32[]{:S(2)}) collective-permute-start(bf16[256,512]{1,0:T(8,128)(2,1)S(1)} %copy-done.5), channel_id=1, source_target_pairs={{0,6},{2,8},{4,10},{6,12},{8,14},{10,16},{12,18},{14,20},{16,22},{... | collective-permute-start | bytes 786440 | tf_op jit(solution)/shard_map/ppermute | solution.py:14
  43.3 27.8 %collective-permute-start.6 = (bf16[256,512]{1,0:T(8,128)(2,1)S(1)}, bf16[256,512]{1,0:T(8,128)(2,1)S(1)}, u32[]{:S(2)}, u32[]{:S(2)}) collective-permute-start(bf16[256,512]{1,0:T(8,128)(2,1)S(1)} %copy-done.5), channel_id=1, source_target_pairs={{0,4},{2,6},{4,8},{6,10},{8,12},{10,14},{12,16},{14,18},{16,20},{1... | collective-permute-start | bytes 786440 | tf_op jit(solution)/shard_map/ppermute | solution.py:14
  48.7 25.3 %collective-permute-start.7 = (bf16[256,512]{1,0:T(8,128)(2,1)S(1)}, bf16[256,512]{1,0:T(8,128)(2,1)S(1)}, u32[]{:S(2)}, u32[]{:S(2)}) collective-permute-start(bf16[256,512]{1,0:T(8,128)(2,1)S(1)} %copy-done.5), channel_id=1, source_target_pairs={{0,2},{2,4},{4,6},{6,8},{8,10},{10,12},{12,14},{14,16},{16,18},{18... | collective-permute-start | bytes 786440 | tf_op jit(solution)/shard_map/ppermute | solution.py:14
  74.1 1.8 copy-start.6
  78.9 1.7 copy-start.7
  84.4 2.1 copy-start.9
  92.5 146.0 %reduce-scatter.5.cloned.1.call-start = ((), (), s32[]{:S(2)}) async-start(), calls=%async_computation.3 | async-start | bytes 4456448 | tf_op jit(solution)/shard_map/reduce_scatter | solution.py:94
  129.4 10.9 %collective-permute-start.10 = (bf16[256,256]{1,0:T(8,128)(2,1)S(1)}, bf16[256,256]{1,0:T(8,128)(2,1)S(1)}, u32[]{:S(2)}, u32[]{:S(2)}) collective-permute-start(bf16[256,256]{1,0:T(8,128)(2,1)S(1)} %get-tuple-element.17), channel_id=1, source_target_pairs={{6,0},{8,2},{10,4},{12,6},{14,8},{16,10},{18,12},{20,14},{22,16},{... | collective-permute-start | bytes 393224 | tf_op jit(solution)/shard_map/ppermute | solution.py:14
  132.3 9.3 %collective-permute-start.11 = (bf16[256,256]{1,0:T(8,128)(2,1)S(1)}, bf16[256,256]{1,0:T(8,128)(2,1)S(1)}, u32[]{:S(2)}, u32[]{:S(2)}) collective-permute-start(bf16[256,256]{1,0:T(8,128)(2,1)S(1)} %get-tuple-element.16), channel_id=1, source_target_pairs={{8,0},{10,2},{12,4},{14,6},{16,8},{18,10},{20,12},{22,14},{24,16},... | collective-permute-start | bytes 393224 | tf_op jit(solution)/shard_map/ppermute | solution.py:14
  134.5 9.6 %collective-permute-start.12 = (bf16[256,256]{1,0:T(8,128)(2,1)S(1)}, bf16[256,256]{1,0:T(8,128)(2,1)S(1)}, u32[]{:S(2)}, u32[]{:S(2)}) collective-permute-start(bf16[256,256]{1,0:T(8,128)(2,1)S(1)} %get-tuple-element.15), channel_id=1, source_target_pairs={{10,0},{12,2},{14,4},{16,6},{18,8},{20,10},{22,12},{24,14},{26,16}... | collective-permute-start | bytes 393224 | tf_op jit(solution)/shard_map/ppermute | solution.py:14
  136.4 10.4 %collective-permute-start.13 = (bf16[256,256]{1,0:T(8,128)(2,1)S(1)}, bf16[256,256]{1,0:T(8,128)(2,1)S(1)}, u32[]{:S(2)}, u32[]{:S(2)}) collective-permute-start(bf16[256,256]{1,0:T(8,128)(2,1)S(1)} %get-tuple-element.14), channel_id=1, source_target_pairs={{12,0},{14,2},{16,4},{18,6},{20,8},{22,10},{24,12},{26,14},{28,16}... | collective-permute-start | bytes 393224 | tf_op jit(solution)/shard_map/ppermute | solution.py:14
  138.3 11.2 %collective-permute-start.14 = (bf16[256,256]{1,0:T(8,128)(2,1)S(1)}, bf16[256,256]{1,0:T(8,128)(2,1)S(1)}, u32[]{:S(2)}, u32[]{:S(2)}) collective-permute-start(bf16[256,256]{1,0:T(8,128)(2,1)S(1)} %get-tuple-element.13), channel_id=1, source_target_pairs={{14,0},{16,2},{18,4},{20,6},{22,8},{24,10},{26,12},{28,14},{30,16}... | collective-permute-start | bytes 393224 | tf_op jit(solution)/shard_map/ppermute | solution.py:14
  140.3 11.0 %collective-permute-start.15 = (bf16[256,256]{1,0:T(8,128)(2,1)S(1)}, bf16[256,256]{1,0:T(8,128)(2,1)S(1)}, u32[]{:S(2)}, u32[]{:S(2)}) collective-permute-start(bf16[256,256]{1,0:T(8,128)(2,1)S(1)} %get-tuple-element.12), channel_id=1, source_target_pairs={{16,0},{18,2},{20,4},{22,6},{24,8},{26,10},{28,12},{30,14},{17,1},... | collective-permute-start | bytes 393224 | tf_op jit(solution)/shard_map/ppermute | solution.py:14
  141.6 22.0 %collective-permute-start.8 = (bf16[256,256]{1,0:T(8,128)(2,1)S(1)}, bf16[256,256]{1,0:T(8,128)(2,1)S(1)}, u32[]{:S(2)}, u32[]{:S(2)}) collective-permute-start(bf16[256,256]{1,0:T(8,128)(2,1)S(1)} %get-tuple-element.11), channel_id=1, source_target_pairs={{2,0},{4,2},{6,4},{8,6},{10,8},{12,10},{14,12},{16,14},{18,16},{20... | collective-permute-start | bytes 393224 | tf_op jit(solution)/shard_map/ppermute | solution.py:14
  144.0 20.6 %collective-permute-start.9 = (bf16[256,256]{1,0:T(8,128)(2,1)S(1)}, bf16[256,256]{1,0:T(8,128)(2,1)S(1)}, u32[]{:S(2)}, u32[]{:S(2)}) collective-permute-start(bf16[256,256]{1,0:T(8,128)(2,1)S(1)} %get-tuple-element.18), channel_id=1, source_target_pairs={{4,0},{6,2},{8,4},{10,6},{12,8},{14,10},{16,12},{18,14},{20,16},{2... | collective-permute-start | bytes 393224 | tf_op jit(solution)/shard_map/ppermute | solution.py:14
  168.5 2.8 %copy-start.8 = (bf16[2304,512]{1,0:T(8,128)(2,1)S(1)}, bf16[2304,512]{1,0:T(8,128)(2,1)}, u32[]{:S(2)}) copy-start(bf16[2304,512]{1,0:T(8,128)(2,1)} %copy-done.6) | copy-start | bytes 7077892
Sparse Core Ops, SparseCore 0:
  92.6 35.3 reduce-scatter.2
  168.6 69.8 reduce-scatter.4
where the time goes:
time: 252 us; the launch traced here: 247 us
  waiting for transfers between devices  130 us (52%)
  local copies, waits for them, and re-layouts  36.4 us (14%)
  starting transfers between devices  35.2 us (14%)
  matrix products  19 us (8%)
  between operations  14.4 us (6%)
  other arithmetic  7.35 us (3%)
  blocking collectives  4.47 us (2%)
    reduce_scatter x1, waiting for transfers between devices, local(): lax.psum_scatter(jnp.einsum('tr,tc->rc', inputs_normed, my_half, preferre...  53 us
    ppermute x16, waiting for transfers between devices, passed_along(): lax.ppermute(value, axis, [(source, source + steps) for source in range(l...  41.8 us
    reduce_scatter x1, waiting for transfers between devices, local(): lax.psum_scatter(blocks.astype(jnp.bfloat16), 'head', scatter_dimension=2...  35.5 us
    ppermute x16, starting transfers between devices, passed_along(): lax.ppermute(value, axis, [(source, source + steps) for source in range(l...  35.1 us
    broadcast_in_dim x3, local copies, waits for them, and re-layouts, attention_block(): masked = jnp.where(allowed[:, None, :], scores, -jnp.inf)  15.9 us
    unnamed x29, local copies, waits for them, and re-layouts  7.48 us
  transfers between devices with their start and end apart: 18, of which 14 were waited for; matrix products, arithmetic and copies ran while one was open for 15% of the time, Pallas kernels for 0%

commit v1 on v0

v1 whole, which is shorter than its diff:
```python
import functools
import math

import jax
import jax.numpy as jnp
from jax import lax
from jax.experimental import pallas as pl
from jax.experimental.pallas import tpu as pltpu
from jax.sharding import PartitionSpec as P

WIN = 2048
MESH = pl.DeviceIdType.MESH
F32 = jnp.float32
BF16 = jnp.bfloat16
NT = (((1,), (1,)), ((), ()))
TN = (((0,), (0,)), ((), ()))


def dot(a, b, dims=(((1,), (0,)), ((), ()))):
    return lax.dot_general(a, b, dims, preferred_element_type=F32)


def kernel(planes, rows_out, heads, norm, q_ref, kv_ref, do_ref, lo_ref, x_hbm, w_hbm,
           dq_ref, ig_ref, wg_ref,
           win, qf, dof, sc, dp, pb, ds, acc, gs, rc, ys, yr, zs, zr, xs, xr, mh, oh,
           xv, wv, xt, wb, wa, cr, yw, ywr, zw, zwr,
           loc_sem, own_sem, zsend, zrecv, ysend, yrecv, csend, crecv,
           gsend, grecv, bysend, byrecv, bzsend, bzrecv, bxsend, bxrecv,
           wcsend, wcrecv, wysend, wyrecv, wzsend, wzrecv):
    tok = q_ref.shape[0]
    hd = kv_ref.shape[1] // 2
    nblk = WIN // tok + 1
    s_idx = lax.axis_index("seq")
    h_idx = lax.axis_index("head")
    k = s_idx % 2
    y = (s_idx // 2) % 2
    p = s_idx // 4
    core_dev = ((p * 2 + y) * 2 + 1 - k, h_idx)
    y_dev = ((p * 2 + 1 - y) * 2 + k, h_idx)
    x_dev = (s_idx, 1 - h_idx)

    def plane_dev(step):
        return ((((p + step) % planes) * 2 + y) * 2 + k, h_idx)

    next_dev = plane_dev(1)
    prev_dev = plane_dev(planes - 1)

    load_x = pltpu.make_async_copy(x_hbm, xv, loc_sem.at[0])
    load_w = pltpu.make_async_copy(w_hbm, wv, loc_sem.at[1])
    load_x.start()
    load_w.start()

    barrier = pltpu.get_barrier_semaphore()
    for dev in [core_dev, y_dev, x_dev] + [plane_dev(t) for t in range(1, planes)]:
        pl.semaphore_signal(barrier, inc=1, device_id=dev, device_id_type=MESH)
    pl.semaphore_wait(barrier, planes + 2)

    def remote(src, dst, ssem, rsem, dev):
        return pltpu.make_async_remote_copy(
            src_ref=src, dst_ref=dst, send_sem=ssem, recv_sem=rsem,
            device_id=dev, device_id_type=MESH)

    def slot(half, j, core):
        return win.at[half, pl.ds(((4 - j) * 2 + core) * tok, tok)]

    def kv_half(half):
        return kv_ref.at[:, pl.ds(half * hd, hd)]

    def z_own(half):
        return remote(kv_half(half), slot(half, 2, k), zsend.at[0, half], zrecv.at[0, half], next_dev)

    def z_relay(half):
        return remote(slot(half, 2, k), slot(half, 4, k), zsend.at[1, half], zrecv.at[1, half], next_dev)

    def y_first(half, src):
        return remote(src, slot(half, 1, k), ysend.at[0, half], yrecv.at[0, half], y_dev)

    def y_second(half, j):
        return remote(slot(half, j, k), slot(half, 3, k), ysend.at[1, half], yrecv.at[1, half], y_dev)

    def to_core(half, j, src):
        return remote(src, slot(half, j, k), csend.at[j, half], crecv.at[j, half], core_dev)

    def own_fill(half):
        return pltpu.make_async_copy(kv_half(half), slot(half, 0, k), own_sem.at[half])

    def sends_core(j):
        return k == 0 if j == 0 else (k == 1 if j == 4 else None)

    def start_core(half, j, src):
        cond = sends_core(j)
        if cond is None:
            to_core(half, j, src).start()
        else:
            pl.when(cond)(lambda: to_core(half, j, src).start())

    for half in range(2):
        z_own(half).start()
        pl.when(y == 0)(lambda half=half: y_first(half, kv_half(half)).start())
        own_fill(half).start()
        start_core(half, 0, kv_half(half))

    for h in range(heads):
        qf[h * tok:(h + 1) * tok, :] = q_ref[:, h * hd:(h + 1) * hd]
        dof[h * tok:(h + 1) * tok, :] = do_ref[:, h * hd:(h + 1) * hd]

    for half in range(2):
        z_own(half).wait_recv()
        z_relay(half).start()

        @pl.when(y == 0)
        def _(half=half):
            y_second(half, 2).start()

        @pl.when(y == 1)
        def _(half=half):
            y_first(half, slot(half, 2, k)).start()

        start_core(half, 2, slot(half, 2, k))

    load_x.wait()
    per = max(1, 256 // rows_out)
    wide = per * rows_out
    for i in range(xv.shape[1] // wide):
        piece = xv[:, i * wide:(i + 1) * wide].T
        for u in range(per):
            dest = i * per + u
            place = ((dest % 2) * 2 + (dest // 2) % 2) * planes + dest // 4
            xt[place * rows_out:(place + 1) * rows_out, :] = piece[u * rows_out:(u + 1) * rows_out]

    for half in range(2):
        y_first(half, kv_half(half)).wait_recv()
        start_core(half, 1, slot(half, 1, k))
    for half in range(2):
        z_relay(half).wait_recv()
        pl.when(y == 1)(lambda half=half: y_second(half, 4).start())
        start_core(half, 4, slot(half, 4, k))
    for half in range(2):
        y_second(half, 2).wait_recv()
        start_core(half, 3, slot(half, 3, k))
    for half in range(2):
        own_fill(half).wait()
        for j in range(1, 4):
            to_core(half, j, slot(half, j, k)).wait_recv()
        pl.when(k == 1)(lambda half=half: to_core(half, 0, slot(half, 0, k)).wait_recv())
        pl.when(k == 0)(lambda half=half: to_core(half, 4, slot(half, 4, k)).wait_recv())

    lo = lo_ref[...]
    hi = lax.broadcasted_iota(jnp.int32, (1, tok), 1) + WIN
    inv_root = 1.0 / math.sqrt(hd)

    def block_rows(d):
        return pl.ds(pl.multiple_of((k + d) * tok, tok), tok)

    def own_rows(d):
        return pl.ds(pl.multiple_of(d * tok, tok), tok)

    def pass_scores(d, tops):
        keys = win[0, block_rows(d), :]
        r = lax.broadcasted_iota(jnp.int32, (tok, tok), 0) + d * tok
        ok = (r >= lo) & (r <= hi)
        out = []
        for h in range(heads):
            s = dot(keys, qf[h * tok:(h + 1) * tok, :], NT) * inv_root
            s = jnp.where(ok, s, -jnp.inf)
            sc[own_rows(d), h * tok:(h + 1) * tok] = s
            out.append(jnp.maximum(tops[h], jnp.max(s, axis=0, keepdims=True)))
        return tuple(out)

    tops = lax.fori_loop(
        0, nblk, pass_scores, tuple(jnp.full((1, tok), -jnp.inf, F32) for _ in range(heads)))

    def pass_exp(d, sums):
        vals = win[1, block_rows(d), :]
        out = []
        for h in range(heads):
            cols = slice(h * tok, (h + 1) * tok)
            e = jnp.exp(sc[own_rows(d), cols] - tops[h])
            g = dot(vals, dof[cols, :], NT)
            sc[own_rows(d), cols] = e
            dp[own_rows(d), cols] = g
            out.append((sums[h][0] + jnp.sum(e, axis=0, keepdims=True),
                        sums[h][1] + jnp.sum(e * g, axis=0, keepdims=True)))
        return tuple(out)

    zero = jnp.zeros((1, tok), F32)
    sums = lax.fori_loop(0, nblk, pass_exp, tuple((zero, zero) for _ in range(heads)))
    invs = [1.0 / total for total, _ in sums]
    deltas = [part * inv for (_, part), inv in zip(sums, invs)]

    def pass_grad(d):
        for h in range(heads):
            cols = slice(h * tok, (h + 1) * tok)
            prob = sc[own_rows(d), cols] * invs[h]
            pb[own_rows(d), cols] = prob.astype(BF16)
            ds[own_rows(d), cols] = (prob * (dp[own_rows(d), cols] - deltas[h])).astype(BF16)

    def grad_of(d, half):
        if half == 0:
            return dot(ds[own_rows(d), :], qf[...]) * inv_root
        return dot(pb[own_rows(d), :], dof[...])

    def g_copy(m, half):
        return remote(gs.at[m, half], rc.at[m, half], gsend.at[m, half], grecv.at[m, half], core_dev)

    def grad_pair(m):
        pass_grad(2 * m + 1)
        for half in range(2):
            gs[m, half] = grad_of(2 * m + 1, half).astype(BF16)
            g_copy(m, half).start()
        pass_grad(2 * m)
        for half in range(2):
            acc[4 - m, half] = grad_of(2 * m, half)

    def add_core(m):
        for half in range(2):
            g_copy(m, half).wait_recv()
            acc[3 - m + k, half] = acc[3 - m + k, half] + rc[m, half].astype(F32)

    def y_copy(i, half):
        return remote(ys.at[i, half], yr.at[i, half], bysend.at[i, half], byrecv.at[i, half], y_dev)

    def z_copy(i, half):
        return remote(zs.at[i, half], zr.at[i, half], bzsend.at[i, half], bzrecv.at[i, half], prev_dev)

    grad_pair(0)
    grad_pair(1)
    grad_pair(2)
    add_core(0)
    add_core(1)
    for half in range(2):
        ys[1, half] = acc[3, half].astype(BF16)
        y_copy(1, half).start()
    grad_pair(3)
    pass_grad(8)
    for half in range(2):
        acc[0, half] = grad_of(8, half)
    add_core(2)
    add_core(3)
    for half in range(2):
        ys[0, half] = acc[1, half].astype(BF16)
        y_copy(0, half).start()
    for half in range(2):
        y_copy(1, half).wait_recv()
        acc[2 + 2 * y, half] = acc[2 + 2 * y, half] + yr[1, half].astype(F32)
        zs[1, half] = acc[4, half].astype(BF16)
        z_copy(1, half).start()
    for h in range(heads):
        cols = slice(h * tok, (h + 1) * tok)
        keys = win[0, pl.ds(pl.multiple_of(k * tok, tok), nblk * tok), :]
        dq_ref[:, h * hd:(h + 1) * hd] = (dot(ds[:, cols], keys, TN) * inv_root).astype(BF16)
    for half in range(2):
        y_copy(0, half).wait_recv()
        acc[2 * y, half] = acc[2 * y, half] + yr[0, half].astype(F32)
        z_copy(1, half).wait_recv()
        zs[0, half] = (acc[2, half] + zr[1, half].astype(F32)).astype(BF16)
        z_copy(0, half).start()
    for half in range(2):
        z_copy(0, half).wait_recv()
        acc[0, half] = acc[0, half] + zr[0, half].astype(F32)

    x_half = remote(xs, xr, bxsend.at[0], bxrecv.at[0], x_dev)
    x_back = remote(mh, oh, bxsend.at[1], bxrecv.at[1], x_dev)
    xs[...] = acc[0, 1 - h_idx].astype(BF16)
    x_half.start()
    x_half.wait_recv()
    mh[...] = (acc[0, h_idx] + xr[...].astype(F32)).astype(BF16)
    x_back.start()

    group = planes * rows_out
    half_rows = 2 * group

    def w_core(i):
        return remote(wb.at[i], cr.at[i], wcsend.at[i], wcrecv.at[i], core_dev)

    def xt_rows(core, yy):
        return xt[pl.ds(pl.multiple_of((core * 2 + yy) * group, group), group), :]

    def w_y(t):
        return remote(yw.at[t], ywr.at[t], wysend.at[t], wyrecv.at[t], y_dev)

    def w_z(t):
        return remote(zw.at[t], zwr.at[t], wzsend.at[t], wzrecv.at[t], plane_dev(t))

    for i in range(2):
        yy = 1 - y if i == 0 else y
        wb[i] = dot(xt_rows(1 - k, yy), mh[...]).astype(BF16)
        w_core(i).start()
    for i in range(2):
        yy = 1 - y if i == 0 else y
        wa[i] = dot(xt_rows(k, yy), mh[...])

    order = list(range(1, planes)) + [0]

    def plane_rows(t):
        return pl.ds(pl.multiple_of(((p + t) % planes) * rows_out, rows_out), rows_out)

    w_core(0).wait_recv()
    for t in order:
        yw[t] = (wa[0, plane_rows(t), :] + cr[0, plane_rows(t), :].astype(F32)).astype(BF16)
        w_y(t).start()
    w_core(1).wait_recv()
    wa[1] = wa[1] + cr[1].astype(F32)

    load_w.wait()
    x_back.wait_recv()
    first = jnp.where(h_idx == 0, mh[...].astype(F32), oh[...].astype(F32)).astype(BF16)
    second = jnp.where(h_idx == 0, oh[...].astype(F32), mh[...].astype(F32)).astype(BF16)
    width = wv.shape[1]
    step = 512
    for i in range(width // step):
        cols = slice(i * step, (i + 1) * step)
        ig_ref[:, cols] = (dot(first, wv[0, cols, :], NT) + dot(second, wv[1, cols, :], NT)).astype(BF16)

    for t in order[:-1]:
        w_y(t).wait_recv()
        zw[t] = (wa[1, plane_rows(t), :] + ywr[t].astype(F32)).astype(BF16)
        w_z(t).start()
    w_y(0).wait_recv()
    total = wa[1, plane_rows(0), :] + ywr[0].astype(F32)
    for t in order[:-1]:
        w_z(t).wait_recv()
        total = total + zwr[t].astype(F32)
    wg_ref[...] = total * norm

    for half in range(2):
        z_own(half).wait_send()
        z_relay(half).wait_send()
        y_first(half, kv_half(half)).wait_send()
        y_second(half, 2).wait_send()
        for j in range(1, 4):
            to_core(half, j, slot(half, j, k)).wait_send()
        pl.when(k == 0)(lambda half=half: to_core(half, 0, slot(half, 0, k)).wait_send())
        pl.when(k == 1)(lambda half=half: to_core(half, 4, slot(half, 4, k)).wait_send())
        for m in range(4):
            g_copy(m, half).wait_send()
        for i in range(2):
            y_copy(i, half).wait_send()
            z_copy(i, half).wait_send()
    x_half.wait_send()
    x_back.wait_send()
    for i in range(2):
        w_core(i).wait_send()
    for t in order:
        w_y(t).wait_send()
    for t in order[:-1]:
        w_z(t).wait_send()


def local(query, key_value, out_grad, inputs_normed, kv_weight, segment_ids):
    tok = query.shape[0]
    hd = key_value.shape[1] // 2
    heads = query.shape[1] // hd
    seqs = lax.axis_size("seq")
    planes = seqs // 4
    width = inputs_normed.shape[1]
    rows_out = width // seqs
    span = WIN + tok
    nblk = span // tok
    group = planes * rows_out
    begin = lax.axis_index("seq") * tok
    padded = jnp.concatenate([jnp.full((WIN,), -1, jnp.int32), segment_ids])
    key_seg = lax.dynamic_slice_in_dim(padded, begin, span, 0)
    earlier = jnp.sum((key_seg[:, None] < key_seg[None, WIN:]).astype(jnp.int32), axis=0)
    lo = jnp.maximum(earlier, jnp.arange(tok, dtype=jnp.int32) + 1)[None]
    norm = 1.0 / math.sqrt(tok * seqs)
    vm = pl.BlockSpec(memory_space=pltpu.VMEM)
    hbm = pl.BlockSpec(memory_space=pl.ANY)
    dma = pltpu.SemaphoreType.DMA
    blk = (tok, hd)
    scratch = [
        pltpu.VMEM((2, (nblk + 1) * tok, hd), BF16),
        pltpu.VMEM((heads * tok, hd), BF16),
        pltpu.VMEM((heads * tok, hd), BF16),
        pltpu.VMEM((span, heads * tok), F32),
        pltpu.VMEM((span, heads * tok), F32),
        pltpu.VMEM((span, heads * tok), BF16),
        pltpu.VMEM((span, heads * tok), BF16),
        pltpu.VMEM((5, 2) + blk, F32),
        pltpu.VMEM((4, 2) + blk, BF16),
        pltpu.VMEM((4, 2) + blk, BF16),
        pltpu.VMEM((2, 2) + blk, BF16),
        pltpu.VMEM((2, 2) + blk, BF16),
        pltpu.VMEM((2, 2) + blk, BF16),
        pltpu.VMEM((2, 2) + blk, BF16),
        pltpu.VMEM(blk, BF16),
        pltpu.VMEM(blk, BF16),
        pltpu.VMEM(blk, BF16),
        pltpu.VMEM(blk, BF16),
        pltpu.VMEM(inputs_normed.shape, BF16),
        pltpu.VMEM(kv_weight.shape, BF16),
        pltpu.VMEM((width, tok), BF16),
        pltpu.VMEM((2, group, hd), BF16),
        pltpu.VMEM((2, group, hd), F32),
        pltpu.VMEM((2, group, hd), BF16),
        pltpu.VMEM((planes, rows_out, hd), BF16),
        pltpu.VMEM((planes, rows_out, hd), BF16),
        pltpu.VMEM((planes, rows_out, hd), BF16),
        pltpu.VMEM((planes, rows_out, hd), BF16),
        dma((2,)), dma((2,)),
        dma((2, 2)), dma((2, 2)), dma((2, 2)), dma((2, 2)), dma((5, 2)), dma((5, 2)),
        dma((4, 2)), dma((4, 2)), dma((2, 2)), dma((2, 2)), dma((2, 2)), dma((2, 2)),
        dma((2,)), dma((2,)),
        dma((2,)), dma((2,)), dma((planes,)), dma((planes,)), dma((planes,)), dma((planes,)),
    ]
    query_grad, input_grad, weight = pl.pallas_call(
        functools.partial(kernel, planes, rows_out, heads, norm),
        out_shape=(
            jax.ShapeDtypeStruct(query.shape, BF16),
            jax.ShapeDtypeStruct((tok, kv_weight.shape[1]), BF16),
            jax.ShapeDtypeStruct((rows_out, hd), F32),
        ),
        in_specs=[vm, vm, vm, vm, hbm, hbm],
        out_specs=(vm, vm, vm),
        scratch_shapes=scratch,
        compiler_params=pltpu.CompilerParams(
            collective_id=0, has_side_effects=True, vmem_limit_bytes=60 * 1024 * 1024),
    )(query, key_value, out_grad, lo, inputs_normed, kv_weight)
    return (query_grad, input_grad, weight[None])


def solution(mesh):
    return jax.shard_map(
        local,
        mesh=mesh,
        in_specs=(
            P("seq", "head"),
            P("seq", None),
            P("seq", "head"),
            P("seq", None),
            P(None, "head", None),
            P(),
        ),
        out_specs=(P("seq", "head"), P("seq", "head"), P("head", "seq", None)),
        check_vma=False,
    )
```

time: 252 us -> 89.7 us (0.36)
  the two profiles are of different devices: /device:TPU:13 before, /device:TPU:9 now
where the time goes in v1:
time: 89.7 us; the launch traced here: 89.4 us
  Pallas kernels  80.7 us (90%)
  local copies, waits for them, and re-layouts  6.47 us (7%)
  other arithmetic  1.63 us (2%)
    pallas_call x1, Pallas kernels, local(): pl.pallas_call(functools.partial(kernel, planes, rows_out, heads, norm),...  80.7 us
    unnamed x5, local copies, waits for them, and re-layouts  4.92 us

profile of v1, /device:TPU:9, one launch (start us, length us, event | category | flops | bytes accessed | tf_op | source)
XLA Modules:
  0.0 89.4 jit_solution(11561115974214224101)
XLA Ops:
  0.6 0.8 pad_dynamic-slice_fusion
  1.4 0.8 pad_dynamic-slice_fusion.1
  2.2 1.1 %convert_reduce_fusion = s32[256]{0:T(256)S(1)} fusion(s32[256]{0:T(256)S(1)} %pad_dynamic-slice_fusion, s32[2304]{0:T(1024)S(1)} %pad_dynamic-slice_fusion.1), kind=kLoop, calls=%fused_computation | loop fusion | flops 1769216 | bytes 11264 | tf_op jit(solution)/shard_map/reduce_sum | solution.py:364
  3.2 0.6 add_maximum_fusion.lo_ref
  3.8 80.7 %shard_map.85 = (bf16[256,1024]{1,0:T(8,128)(2,1)}, bf16[256,2048]{1,0:T(8,128)(2,1)}, f32[256,256]{1,0:T(8,128)}) custom-call(bf16[256,1024]{1,0:T(8,128)(2,1)} %q_ref.1, bf16[256,512]{1,0:T(8,128)(2,1)} %kv_ref.1, bf16[256,1024]{1,0:T(8,128)(2,1)} %do_ref.1, s32[1,256]{1,0:T(1,128)} %add_maximum_fusion.lo_ref, bf16[256,4096]{1,0:T(8,128)(2,1)} %x_hbm.1, ...), custom_call_target="tpu_custom_call" | custom-call | tf_op jit(solution)/shard_map/pallas_call | solution.py:406
  84.5 0.0 copy-start
  84.5 1.9 %copy.12 = bf16[256,1024]{1,0:T(8,128)(2,1)} copy(bf16[256,1024]{1,0:T(8,128)(2,1)} %get-tuple-element.12) | data formatting | bytes 1048576
  86.4 2.3 %copy.13 = bf16[256,2048]{1,0:T(8,128)(2,1)} copy(bf16[256,2048]{1,0:T(8,128)(2,1)} %get-tuple-element.13) | data formatting | bytes 2097152
  88.7 0.0 copy-done
  88.7 0.7 copy.14
Async XLA Ops:
  84.5 4.2 %copy-start = (f32[256,256]{1,0:T(8,128)S(1)}, f32[256,256]{1,0:T(8,128)}, u32[]{:S(2)}) copy-start(f32[256,256]{1,0:T(8,128)} %get-tuple-element.8) | copy-start | bytes 786436

commit v2 on v1

--- a/solution.py
+++ b/solution.py
@@ -20,9 +20,9 @@
     return lax.dot_general(a, b, dims, preferred_element_type=F32)
 
 
-def kernel(planes, rows_out, heads, norm, q_ref, kv_ref, do_ref, lo_ref, x_hbm, w_hbm,
+def kernel(planes, rows_out, heads, norm, q_ref, kv_ref, do_ref, seg_ref, x_hbm, w_hbm,
            dq_ref, ig_ref, wg_ref,
-           win, qf, dof, sc, dp, pb, ds, acc, gs, rc, ys, yr, zs, zr, xs, xr, mh, oh,
+           win, qf, dof, top, sc, dp, pb, ds, acc, gs, rc, ys, yr, zs, zr, xs, xr, mh, oh,
            xv, wv, xt, wb, wa, cr, yw, ywr, zw, zwr,
            loc_sem, own_sem, zsend, zrecv, ysend, yrecv, csend, crecv,
            gsend, grecv, bysend, byrecv, bzsend, bzrecv, bxsend, bxrecv,
@@ -104,6 +104,70 @@
         qf[h * tok:(h + 1) * tok, :] = q_ref[:, h * hd:(h + 1) * hd]
         dof[h * tok:(h + 1) * tok, :] = do_ref[:, h * hd:(h + 1) * hd]
 
+    seg_q = seg_ref[s_idx].astype(F32)
+    earlier = jnp.zeros((1, tok), F32)
+    for d in range(nblk):
+        blk = s_idx - (nblk - 1) + d
+        seg_k = seg_ref[jnp.maximum(blk, 0)].astype(F32)
+        down = jnp.broadcast_to(seg_k, (tok, tok)).T
+        less = jnp.sum((down < seg_q).astype(F32), axis=0, keepdims=True)
+        earlier = earlier + jnp.where(blk >= 0, less, float(tok))
+    col = lax.broadcasted_iota(jnp.int32, (1, tok), 1)
+    lo = jnp.maximum(earlier.astype(jnp.int32), col + 1)
+    hi = col + WIN
+    inv_root = 1.0 / math.sqrt(hd)
+    top[...] = jnp.full(top.shape, -jnp.inf, F32)
+
+    def block_rows(d):
+        return pl.ds(pl.multiple_of((k + d) * tok, tok), tok)
+
+    def own_rows(d):
+        return pl.ds(pl.multiple_of(d * tok, tok), tok)
+
+    def block_scores(d):
+        keys = win[0, block_rows(d), :]
+        vals = win[1, block_rows(d), :]
+        r = lax.broadcasted_iota(jnp.int32, (tok, tok), 0) + d * tok
+        ok = (r >= lo) & (r <= hi)
+        for h in range(heads):
+            cols = slice(h * tok, (h + 1) * tok)
+            s = jnp.where(ok, dot(keys, qf[cols, :], NT) * inv_root, -jnp.inf)
+            sc[own_rows(d), cols] = s
+            top[:, cols] = jnp.maximum(top[:, cols], jnp.max(s, axis=0, keepdims=True))
+            dp[own_rows(d), cols] = dot(vals, dof[cols, :], NT)
+
+    def own_scores(j):
+        block_scores(8 - 2 * j)
+
+    def partner_scores(j):
+        def run():
+            for half in range(2):
+                to_core(half, j, slot(half, j, k)).wait_recv()
+            block_scores(9 - 2 * j - 2 * k)
+
+        if j == 0:
+            pl.when(k == 1)(run)
+        elif j == 4:
+            pl.when(k == 0)(run)
+        else:
+            run()
+
+    per = max(1, 256 // rows_out)
+    wide = per * rows_out
+    pieces = xv.shape[1] // wide
+
+    def transpose_inputs(first, last):
+        for i in range(first, last):
+            piece = xv[:, i * wide:(i + 1) * wide].T
+            for u in range(per):
+                dest = i * per + u
+                place = ((dest % 2) * 2 + (dest // 2) % 2) * planes + dest // 4
+                xt[place * rows_out:(place + 1) * rows_out, :] = piece[u * rows_out:(u + 1) * rows_out]
+
+    for half in range(2):
+        own_fill(half).wait()
+    own_scores(0)
+    partner_scores(0)
     for half in range(2):
         z_own(half).wait_recv()
         z_relay(half).start()
@@ -117,70 +181,38 @@
             y_first(half, slot(half, 2, k)).start()
 
         start_core(half, 2, slot(half, 2, k))
-
+    own_scores(2)
     load_x.wait()
-    per = max(1, 256 // rows_out)
-    wide = per * rows_out
-    for i in range(xv.shape[1] // wide):
-        piece = xv[:, i * wide:(i + 1) * wide].T
-        for u in range(per):
-            dest = i * per + u
-            place = ((dest % 2) * 2 + (dest // 2) % 2) * planes + dest // 4
-            xt[place * rows_out:(place + 1) * rows_out, :] = piece[u * rows_out:(u + 1) * rows_out]
-
+    transpose_inputs(0, pieces // 2)
     for half in range(2):
         y_first(half, kv_half(half)).wait_recv()
         start_core(half, 1, slot(half, 1, k))
+    partner_scores(2)
+    own_scores(1)
     for half in range(2):
         z_relay(half).wait_recv()
         pl.when(y == 1)(lambda half=half: y_second(half, 4).start())
         start_core(half, 4, slot(half, 4, k))
+    own_scores(4)
+    partner_scores(1)
+    transpose_inputs(pieces // 2, pieces)
+    partner_scores(4)
     for half in range(2):
         y_second(half, 2).wait_recv()
         start_core(half, 3, slot(half, 3, k))
-    for half in range(2):
-        own_fill(half).wait()
-        for j in range(1, 4):
-            to_core(half, j, slot(half, j, k)).wait_recv()
-        pl.when(k == 1)(lambda half=half: to_core(half, 0, slot(half, 0, k)).wait_recv())
-        pl.when(k == 0)(lambda half=half: to_core(half, 4, slot(half, 4, k)).wait_recv())
-
-    lo = lo_ref[...]
-    hi = lax.broadcasted_iota(jnp.int32, (1, tok), 1) + WIN
-    inv_root = 1.0 / math.sqrt(hd)
-
-    def block_rows(d):
-        return pl.ds(pl.multiple_of((k + d) * tok, tok), tok)
-
-    def own_rows(d):
-        return pl.ds(pl.multiple_of(d * tok, tok), tok)
-
-    def pass_scores(d, tops):
-        keys = win[0, block_rows(d), :]
-        r = lax.broadcasted_iota(jnp.int32, (tok, tok), 0) + d * tok
-        ok = (r >= lo) & (r <= hi)
-        out = []
-        for h in range(heads):
-            s = dot(keys, qf[h * tok:(h + 1) * tok, :], NT) * inv_root
-            s = jnp.where(ok, s, -jnp.inf)
-            sc[own_rows(d), h * tok:(h + 1) * tok] = s
-            out.append(jnp.maximum(tops[h], jnp.max(s, axis=0, keepdims=True)))
-        return tuple(out)
-
-    tops = lax.fori_loop(
-        0, nblk, pass_scores, tuple(jnp.full((1, tok), -jnp.inf, F32) for _ in range(heads)))
+    own_scores(3)
+    partner_scores(3)
+
+    tops = [top[:, h * tok:(h + 1) * tok] for h in range(heads)]
 
     def pass_exp(d, sums):
-        vals = win[1, block_rows(d), :]
         out = []
         for h in range(heads):
             cols = slice(h * tok, (h + 1) * tok)
             e = jnp.exp(sc[own_rows(d), cols] - tops[h])
-            g = dot(vals, dof[cols, :], NT)
             sc[own_rows(d), cols] = e
-            dp[own_rows(d), cols] = g
             out.append((sums[h][0] + jnp.sum(e, axis=0, keepdims=True),
-                        sums[h][1] + jnp.sum(e * g, axis=0, keepdims=True)))
+                        sums[h][1] + jnp.sum(e * dp[own_rows(d), cols], axis=0, keepdims=True)))
         return tuple(out)
 
     zero = jnp.zeros((1, tok), F32)
@@ -203,69 +235,94 @@
     def g_copy(m, half):
         return remote(gs.at[m, half], rc.at[m, half], gsend.at[m, half], grecv.at[m, half], core_dev)
 
-    def grad_pair(m):
+    def send_grad(m):
         pass_grad(2 * m + 1)
         for half in range(2):
             gs[m, half] = grad_of(2 * m + 1, half).astype(BF16)
             g_copy(m, half).start()
-        pass_grad(2 * m)
+
+    def own_grad(j):
+        pass_grad(8 - 2 * j)
         for half in range(2):
-            acc[4 - m, half] = grad_of(2 * m, half)
-
-    def add_core(m):
-        for half in range(2):
-            g_copy(m, half).wait_recv()
-            acc[3 - m + k, half] = acc[3 - m + k, half] + rc[m, half].astype(F32)
-
-    def y_copy(i, half):
-        return remote(ys.at[i, half], yr.at[i, half], bysend.at[i, half], byrecv.at[i, half], y_dev)
-
-    def z_copy(i, half):
-        return remote(zs.at[i, half], zr.at[i, half], bzsend.at[i, half], bzrecv.at[i, half], prev_dev)
-
-    grad_pair(0)
-    grad_pair(1)
-    grad_pair(2)
-    add_core(0)
-    add_core(1)
-    for half in range(2):
-        ys[1, half] = acc[3, half].astype(BF16)
-        y_copy(1, half).start()
-    grad_pair(3)
-    pass_grad(8)
-    for half in range(2):
-        acc[0, half] = grad_of(8, half)
-    add_core(2)
-    add_core(3)
-    for half in range(2):
-        ys[0, half] = acc[1, half].astype(BF16)
-        y_copy(0, half).start()
-    for half in range(2):
-        y_copy(1, half).wait_recv()
-        acc[2 + 2 * y, half] = acc[2 + 2 * y, half] + yr[1, half].astype(F32)
-        zs[1, half] = acc[4, half].astype(BF16)
-        z_copy(1, half).start()
-    for h in range(heads):
+            acc[j, half] = grad_of(8 - 2 * j, half)
+
+    def x_copy(j):
+        return remote(xs.at[j], xr.at[j], bxsend.at[j], bxrecv.at[j], x_dev)
+
+    def y_copy(i):
+        return remote(ys.at[i], yr.at[i], bysend.at[i], byrecv.at[i], y_dev)
+
+    def z_copy(i):
+        return remote(zs.at[i], zr.at[i], bzsend.at[i], bzrecv.at[i], prev_dev)
+
+    def to_x(j):
+        def add():
+            m = 3 + k - j if 0 < j < 4 else (0 if j == 4 else 3)
+            for half in range(2):
+                g_copy(m, half).wait_recv()
+                acc[j, half] = acc[j, half] + rc[m, half].astype(F32)
+
+        if j == 0:
+            pl.when(k == 0)(add)
+        elif j == 4:
+            pl.when(k == 1)(add)
+        else:
+            add()
+        xs[j] = acc[j, 1 - h_idx].astype(BF16)
+        x_copy(j).start()
+
+    def from_x(j):
+        x_copy(j).wait_recv()
+        acc[j, h_idx] = acc[j, h_idx] + xr[j].astype(F32)
+
+    def to_y(i, j):
+        from_x(j)
+        ys[i] = acc[j, h_idx].astype(BF16)
+        y_copy(i).start()
+
+    def from_y(i):
+        y_copy(i).wait_recv()
+        acc[2 * i + 2 * y, h_idx] = acc[2 * i + 2 * y, h_idx] + yr[i].astype(F32)
+
+    send_grad(1 - k)
+    own_grad(3)
+    send_grad(3 - k)
+    to_x(3)
+    own_grad(1)
+    send_grad(3 * k)
+    to_x(1)
+    own_grad(4)
+    send_grad(2 - k)
+    to_x(4)
+    own_grad(2)
+    to_x(2)
+    own_grad(0)
+    to_x(0)
+    to_y(1, 3)
+    to_y(0, 1)
+    keys_all = win[0, pl.ds(pl.multiple_of(k * tok, tok), nblk * tok), :]
+
+    def query_part(h):
         cols = slice(h * tok, (h + 1) * tok)
-        keys = win[0, pl.ds(pl.multiple_of(k * tok, tok), nblk * tok), :]
-        dq_ref[:, h * hd:(h + 1) * hd] = (dot(ds[:, cols], keys, TN) * inv_root).astype(BF16)
-    for half in range(2):
-        y_copy(0, half).wait_recv()
-        acc[2 * y, half] = acc[2 * y, half] + yr[0, half].astype(F32)
-        z_copy(1, half).wait_recv()
-        zs[0, half] = (acc[2, half] + zr[1, half].astype(F32)).astype(BF16)
-        z_copy(0, half).start()
-    for half in range(2):
-        z_copy(0, half).wait_recv()
-        acc[0, half] = acc[0, half] + zr[0, half].astype(F32)
-
-    x_half = remote(xs, xr, bxsend.at[0], bxrecv.at[0], x_dev)
-    x_back = remote(mh, oh, bxsend.at[1], bxrecv.at[1], x_dev)
-    xs[...] = acc[0, 1 - h_idx].astype(BF16)
-    x_half.start()
-    x_half.wait_recv()
-    mh[...] = (acc[0, h_idx] + xr[...].astype(F32)).astype(BF16)
-    x_back.start()
+        dq_ref[:, h * hd:(h + 1) * hd] = (dot(ds[:, cols], keys_all, TN) * inv_root).astype(BF16)
+
+    for h in range(heads // 2):
+        query_part(h)
+    from_x(4)
+    from_x(2)
+    from_y(1)
+    zs[1] = acc[4, h_idx].astype(BF16)
+    z_copy(1).start()
+    for h in range(heads // 2, heads):
+        query_part(h)
+    from_x(0)
+    from_y(0)
+    z_copy(1).wait_recv()
+    zs[0] = (acc[2, h_idx] + zr[1].astype(F32)).astype(BF16)
+    z_copy(0).start()
+    z_copy(0).wait_recv()
+    mh[...] = (acc[0, h_idx] + zr[0].astype(F32)).astype(BF16)
+    x_back = remote(mh, oh, bxsend.at[5], bxrecv.at[5], x_dev)
 
     group = planes * rows_out
     half_rows = 2 * group
@@ -286,6 +343,7 @@
         yy = 1 - y if i == 0 else y
         wb[i] = dot(xt_rows(1 - k, yy), mh[...]).astype(BF16)
         w_core(i).start()
+    x_back.start()
     for i in range(2):
         yy = 1 - y if i == 0 else y
         wa[i] = dot(xt_rows(k, yy), mh[...])
@@ -334,10 +392,11 @@
         pl.when(k == 1)(lambda half=half: to_core(half, 4, slot(half, 4, k)).wait_send())
         for m in range(4):
             g_copy(m, half).wait_send()
-        for i in range(2):
-            y_copy(i, half).wait_send()
-            z_copy(i, half).wait_send()
-    x_half.wait_send()
+    for i in range(2):
+        y_copy(i).wait_send()
+        z_copy(i).wait_send()
+    for j in range(5):
+        x_copy(j).wait_send()
     x_back.wait_send()
     for i in range(2):
         w_core(i).wait_send()
@@ -345,6 +404,16 @@
         w_y(t).wait_send()
     for t in order[:-1]:
         w_z(t).wait_send()
+
+
+def put_out(a_ref, b_ref, c_ref, a_out, b_out, c_out, sem):
+    copies = [pltpu.make_async_copy(a_ref, a_out, sem.at[0]),
+              pltpu.make_async_copy(b_ref, b_out, sem.at[1]),
+              pltpu.make_async_copy(c_ref, c_out, sem.at[2])]
+    for copy in copies:
+        copy.start()
+    for copy in copies:
+        copy.wait()
 
 
 def local(query, key_value, out_grad, inputs_normed, kv_weight, segment_ids):
@@ -358,11 +427,7 @@
     span = WIN + tok
     nblk = span // tok
     group = planes * rows_out
-    begin = lax.axis_index("seq") * tok
-    padded = jnp.concatenate([jnp.full((WIN,), -1, jnp.int32), segment_ids])
-    key_seg = lax.dynamic_slice_in_dim(padded, begin, span, 0)
-    earlier = jnp.sum((key_seg[:, None] < key_seg[None, WIN:]).astype(jnp.int32), axis=0)
-    lo = jnp.maximum(earlier, jnp.arange(tok, dtype=jnp.int32) + 1)[None]
+    seg = segment_ids.reshape(seqs, 1, tok)
     norm = 1.0 / math.sqrt(tok * seqs)
     vm = pl.BlockSpec(memory_space=pltpu.VMEM)
     hbm = pl.BlockSpec(memory_space=pl.ANY)
@@ -372,6 +437,7 @@
         pltpu.VMEM((2, (nblk + 1) * tok, hd), BF16),
         pltpu.VMEM((heads * tok, hd), BF16),
         pltpu.VMEM((heads * tok, hd), BF16),
+        pltpu.VMEM((1, heads * tok), F32),
         pltpu.VMEM((span, heads * tok), F32),
         pltpu.VMEM((span, heads * tok), F32),
         pltpu.VMEM((span, heads * tok), BF16),
@@ -379,12 +445,12 @@
         pltpu.VMEM((5, 2) + blk, F32),
         pltpu.VMEM((4, 2) + blk, BF16),
         pltpu.VMEM((4, 2) + blk, BF16),
-        pltpu.VMEM((2, 2) + blk, BF16),
-        pltpu.VMEM((2, 2) + blk, BF16),
-        pltpu.VMEM((2, 2) + blk, BF16),
-        pltpu.VMEM((2, 2) + blk, BF16),
-        pltpu.VMEM(blk, BF16),
-        pltpu.VMEM(blk, BF16),
+        pltpu.VMEM((2,) + blk, BF16),
+        pltpu.VMEM((2,) + blk, BF16),
+        pltpu.VMEM((2,) + blk, BF16),
+        pltpu.VMEM((2,) + blk, BF16),
+        pltpu.VMEM((5,) + blk, BF16),
+        pltpu.VMEM((5,) + blk, BF16),
         pltpu.VMEM(blk, BF16),
         pltpu.VMEM(blk, BF16),
         pltpu.VMEM(inputs_normed.shape, BF16),
@@ -399,8 +465,8 @@
         pltpu.VMEM((planes, rows_out, hd), BF16),
         dma((2,)), dma((2,)),
         dma((2, 2)), dma((2, 2)), dma((2, 2)), dma((2, 2)), dma((5, 2)), dma((5, 2)),
-        dma((4, 2)), dma((4, 2)), dma((2, 2)), dma((2, 2)), dma((2, 2)), dma((2, 2)),
-        dma((2,)), dma((2,)),
+        dma((4, 2)), dma((4, 2)), dma((2,)), dma((2,)), dma((2,)), dma((2,)),
+        dma((6,)), dma((6,)),
         dma((2,)), dma((2,)), dma((planes,)), dma((planes,)), dma((planes,)), dma((planes,)),
     ]
     query_grad, input_grad, weight = pl.pallas_call(
@@ -415,7 +481,15 @@
         scratch_shapes=scratch,
         compiler_params=pltpu.CompilerParams(
             collective_id=0, has_side_effects=True, vmem_limit_bytes=60 * 1024 * 1024),
-    )(query, key_value, out_grad, lo, inputs_normed, kv_weight)
+    )(query, key_value, out_grad, seg, inputs_normed, kv_weight)
+    results = (query_grad, input_grad, weight)
+    query_grad, input_grad, weight = pl.pallas_call(
+        put_out,
+        out_shape=tuple(jax.ShapeDtypeStruct(r.shape, r.dtype) for r in results),
+        in_specs=[vm, vm, vm],
+        out_specs=(hbm, hbm, hbm),
+        scratch_shapes=[dma((3,))],
+    )(*results)
     return (query_grad, input_grad, weight[None])
 
 

time: 89.7 us -> 77.9 us (0.87)
  the two profiles are of different devices: /device:TPU:9 before, /device:TPU:13 now
where the time goes in v2:
time: 77.9 us; the launch traced here: 77.7 us
  Pallas kernels  76.9 us (99%)
  between operations  0.8 us (1%)
    pallas_call x1, Pallas kernels, local(): pl.pallas_call(functools.partial(kernel, planes, rows_out, heads, norm),...  74.3 us
    pallas_call x1, Pallas kernels, local(): pl.pallas_call(put_out, out_shape=tuple((jax.ShapeDtypeStruct(r.shape, r....  2.67 us

profile of v2, /device:TPU:13, one launch (start us, length us, event | category | flops | bytes accessed | tf_op | source)
XLA Modules:
  0.0 77.7 jit_solution(4182758021606451328)
XLA Ops:
  0.6 74.3 %shard_map.85 = (bf16[256,1024]{1,0:T(8,128)(2,1)}, bf16[256,2048]{1,0:T(8,128)(2,1)}, f32[256,256]{1,0:T(8,128)}) custom-call(bf16[256,1024]{1,0:T(8,128)(2,1)} %q_ref.1, bf16[256,512]{1,0:T(8,128)(2,1)} %kv_ref.1, bf16[256,1024]{1,0:T(8,128)(2,1)} %do_ref.1, s32[16,1,256]{2,1,0:T(1,128)} %bitcast.2, bf16[256,4096]{1,0:T(8,128)(2,1)} %x_hbm.1, ...), custom_call_target="tpu_custom_call" | custom-call | tf_op jit(solution)/shard_map/pallas_call | solution.py:472
  74.9 2.7 %shard_map.86 = (bf16[256,1024]{1,0:T(8,128)(2,1)}, bf16[256,2048]{1,0:T(8,128)(2,1)}, f32[256,256]{1,0:T(8,128)}) custom-call(bf16[256,1024]{1,0:T(8,128)(2,1)} %get-tuple-element.9.a_ref, bf16[256,2048]{1,0:T(8,128)(2,1)} %get-tuple-element.10.b_ref, f32[256,256]{1,0:T(8,128)} %get-tuple-element.11.c_ref), custom_call_target="tpu_custom_call" | custom-call | tf_op jit(solution)/shard_map/pallas_call | solution.py:486

commit v3 on v2

--- a/solution.py
+++ b/solution.py
@@ -23,11 +23,11 @@
 def kernel(planes, rows_out, heads, norm, q_ref, kv_ref, do_ref, seg_ref, x_hbm, w_hbm,
            dq_ref, ig_ref, wg_ref,
            win, qf, dof, top, sc, dp, pb, ds, acc, gs, rc, ys, yr, zs, zr, xs, xr, mh, oh,
-           xv, wv, xt, wb, wa, cr, yw, ywr, zw, zwr,
-           loc_sem, own_sem, zsend, zrecv, ysend, yrecv, csend, crecv,
+           xv, wv, xt, wb, wa, cr, yw, ywr, zw, zwr, dqv, igv,
+           loc_sem, in_sem, own_sem, zsend, zrecv, ysend, yrecv, csend, crecv,
            gsend, grecv, bysend, byrecv, bzsend, bzrecv, bxsend, bxrecv,
            wcsend, wcrecv, wysend, wyrecv, wzsend, wzrecv):
-    tok = q_ref.shape[0]
+    tok = kv_ref.shape[0]
     hd = kv_ref.shape[1] // 2
     nblk = WIN // tok + 1
     s_idx = lax.axis_index("seq")
@@ -47,8 +47,17 @@
 
     load_x = pltpu.make_async_copy(x_hbm, xv, loc_sem.at[0])
     load_w = pltpu.make_async_copy(w_hbm, wv, loc_sem.at[1])
+    loads = []
+    for h in range(heads):
+        for i, (src, dst) in enumerate(((q_ref, qf), (do_ref, dof))):
+            loads.append(pltpu.make_async_copy(
+                src.at[:, pl.ds(h * hd, hd)], dst.at[pl.ds(h * tok, tok)], in_sem.at[i, h]))
+    for load in loads:
+        load.start()
     load_x.start()
     load_w.start()
+    put_q = pltpu.make_async_copy(dqv, dq_ref, loc_sem.at[2])
+    put_i = pltpu.make_async_copy(igv, ig_ref, loc_sem.at[3])
 
     barrier = pltpu.get_barrier_semaphore()
     for dev in [core_dev, y_dev, x_dev] + [plane_dev(t) for t in range(1, planes)]:
@@ -99,10 +108,6 @@
         pl.when(y == 0)(lambda half=half: y_first(half, kv_half(half)).start())
         own_fill(half).start()
         start_core(half, 0, kv_half(half))
-
-    for h in range(heads):
-        qf[h * tok:(h + 1) * tok, :] = q_ref[:, h * hd:(h + 1) * hd]
-        dof[h * tok:(h + 1) * tok, :] = do_ref[:, h * hd:(h + 1) * hd]
 
     seg_q = seg_ref[s_idx].astype(F32)
     earlier = jnp.zeros((1, tok), F32)
@@ -164,6 +169,8 @@
                 place = ((dest % 2) * 2 + (dest // 2) % 2) * planes + dest // 4
                 xt[place * rows_out:(place + 1) * rows_out, :] = piece[u * rows_out:(u + 1) * rows_out]
 
+    for load in loads:
+        load.wait()
     for half in range(2):
         own_fill(half).wait()
     own_scores(0)
@@ -304,7 +311,7 @@
 
     def query_part(h):
         cols = slice(h * tok, (h + 1) * tok)
-        dq_ref[:, h * hd:(h + 1) * hd] = (dot(ds[:, cols], keys_all, TN) * inv_root).astype(BF16)
+        dqv[:, h * hd:(h + 1) * hd] = (dot(ds[:, cols], keys_all, TN) * inv_root).astype(BF16)
 
     for h in range(heads // 2):
         query_part(h)
@@ -315,6 +322,7 @@
     z_copy(1).start()
     for h in range(heads // 2, heads):
         query_part(h)
+    put_q.start()
     from_x(0)
     from_y(0)
     z_copy(1).wait_recv()
@@ -368,8 +376,9 @@
     step = 512
     for i in range(width // step):
         cols = slice(i * step, (i + 1) * step)
-        ig_ref[:, cols] = (dot(first, wv[0, cols, :], NT) + dot(second, wv[1, cols, :], NT)).astype(BF16)
-
+        igv[:, cols] = (dot(first, wv[0, cols, :], NT) + dot(second, wv[1, cols, :], NT)).astype(BF16)
+
+    put_i.start()
     for t in order[:-1]:
         w_y(t).wait_recv()
         zw[t] = (wa[1, plane_rows(t), :] + ywr[t].astype(F32)).astype(BF16)
@@ -381,6 +390,8 @@
         total = total + zwr[t].astype(F32)
     wg_ref[...] = total * norm
 
+    put_q.wait()
+    put_i.wait()
     for half in range(2):
         z_own(half).wait_send()
         z_relay(half).wait_send()
@@ -406,14 +417,24 @@
         w_z(t).wait_send()
 
 
-def put_out(a_ref, b_ref, c_ref, a_out, b_out, c_out, sem):
-    copies = [pltpu.make_async_copy(a_ref, a_out, sem.at[0]),
-              pltpu.make_async_copy(b_ref, b_out, sem.at[1]),
-              pltpu.make_async_copy(c_ref, c_out, sem.at[2])]
-    for copy in copies:
-        copy.start()
-    for copy in copies:
-        copy.wait()
+def put_out(*refs):
+    sources, results, buffers, sems = refs[:3], refs[3:6], refs[6:9], refs[9]
+    fills, drains = [], []
+    for i in range(3):
+        half = sources[i].shape[0] // 2
+        for j in range(2):
+            part = pl.ds(j * half, half)
+            fills.append(pltpu.make_async_copy(
+                sources[i].at[part], buffers[i].at[part], sems.at[0, i, j]))
+            drains.append(pltpu.make_async_copy(
+                buffers[i].at[part], results[i].at[part], sems.at[1, i, j]))
+    for fill in fills:
+        fill.start()
+    for fill, drain in zip(fills, drains):
+        fill.wait()
+        drain.start()
+    for drain in drains:
+        drain.wait()
 
 
 def local(query, key_value, out_grad, inputs_normed, kv_weight, segment_ids):
@@ -463,7 +484,9 @@
         pltpu.VMEM((planes, rows_out, hd), BF16),
         pltpu.VMEM((planes, rows_out, hd), BF16),
         pltpu.VMEM((planes, rows_out, hd), BF16),
-        dma((2,)), dma((2,)),
+        pltpu.VMEM(query.shape, BF16),
+        pltpu.VMEM((tok, kv_weight.shape[1]), BF16),
+        dma((4,)), dma((2, heads)), dma((2,)),
         dma((2, 2)), dma((2, 2)), dma((2, 2)), dma((2, 2)), dma((5, 2)), dma((5, 2)),
         dma((4, 2)), dma((4, 2)), dma((2,)), dma((2,)), dma((2,)), dma((2,)),
         dma((6,)), dma((6,)),
@@ -476,8 +499,8 @@
             jax.ShapeDtypeStruct((tok, kv_weight.shape[1]), BF16),
             jax.ShapeDtypeStruct((rows_out, hd), F32),
         ),
-        in_specs=[vm, vm, vm, vm, hbm, hbm],
-        out_specs=(vm, vm, vm),
+        in_specs=[hbm, vm, hbm, vm, hbm, hbm],
+        out_specs=(hbm, hbm, vm),
         scratch_shapes=scratch,
         compiler_params=pltpu.CompilerParams(
             collective_id=0, has_side_effects=True, vmem_limit_bytes=60 * 1024 * 1024),
@@ -486,9 +509,9 @@
     query_grad, input_grad, weight = pl.pallas_call(
         put_out,
         out_shape=tuple(jax.ShapeDtypeStruct(r.shape, r.dtype) for r in results),
-        in_specs=[vm, vm, vm],
+        in_specs=[hbm, hbm, hbm],
         out_specs=(hbm, hbm, hbm),
-        scratch_shapes=[dma((3,))],
+        scratch_shapes=[pltpu.VMEM(r.shape, r.dtype) for r in results] + [dma((2, 3, 2))],
     )(*results)
     return (query_grad, input_grad, weight[None])
 

time: 77.9 us -> 76.8 us (0.986)
  Pallas kernels: 76.9 us -> 75.8 us
    pallas_call x1, Pallas kernels: 74.3 us -> 73.5 us  [local(): pl.pallas_call(functools.partial(kernel, planes, rows_out, heads, norm),...]
where the time goes in v3:
time: 76.8 us; the launch traced here: 76.6 us
  Pallas kernels  75.8 us (99%)
  between operations  0.8 us (1%)
    pallas_call x1, Pallas kernels, local(): pl.pallas_call(functools.partial(kernel, planes, rows_out, heads, norm),...  73.5 us
    pallas_call x1, Pallas kernels, local(): pl.pallas_call(put_out, out_shape=tuple((jax.ShapeDtypeStruct(r.shape, r....  2.35 us

profile of v3, /device:TPU:13, one launch (start us, length us, event | category | flops | bytes accessed | tf_op | source)
XLA Modules:
  0.0 76.6 jit_solution(7575715713829439865)
XLA Ops:
  0.6 73.5 %shard_map.85 = (bf16[256,1024]{1,0:T(8,128)(2,1)}, bf16[256,2048]{1,0:T(8,128)(2,1)}, f32[256,256]{1,0:T(8,128)}) custom-call(bf16[256,1024]{1,0:T(8,128)(2,1)} %q_ref.1, bf16[256,512]{1,0:T(8,128)(2,1)} %kv_ref.1, bf16[256,1024]{1,0:T(8,128)(2,1)} %do_ref.1, s32[16,1,256]{2,1,0:T(1,128)} %bitcast.2, bf16[256,4096]{1,0:T(8,128)(2,1)} %x_hbm.1, ...), custom_call_target="tpu_custom_call" | custom-call | tf_op jit(solution)/shard_map/pallas_call | solution.py:495
  74.1 2.4 %shard_map.86 = (bf16[256,1024]{1,0:T(8,128)(2,1)}, bf16[256,2048]{1,0:T(8,128)(2,1)}, f32[256,256]{1,0:T(8,128)}) custom-call(bf16[256,1024]{1,0:T(8,128)(2,1)} %get-tuple-element.9.refs_0_, bf16[256,2048]{1,0:T(8,128)(2,1)} %get-tuple-element.10.refs_1_, f32[256,256]{1,0:T(8,128)} %get-tuple-element.11.refs_2_), custom_call_target="tpu_custom_call" | custom-call | tf_op jit(solution)/shard_map/pallas_call | solution.py:509
